TPU v7x, 32 devices: a whole 2x2x4 slice. The times are simulated.
32 devices in a mesh: group: 8 (over y, x, core), shard: 4 (over z).
Axes of the slice: x: 2, y: 2, z: 4, core: 2. Of those that a mesh axis runs over, the one named last changes fastest.
Arguments:
- momentum: bfloat16 [8, 7168, 2048], P(None, ('group', 'shard'))
- gradient: bfloat16 [8, 7168, 2048], P(None, ('group', 'shard'))
- q_prev: bfloat16 [8, 3, 2048, 128], P('group', None, 'shard'), may hold values from -6 to 6
- owner_group: int32 [8], replicated, may hold values from 0 to 7, as said below
- group_counts: int32 [8], replicated, may hold values from 0 to 3, as said below
Outputs:
- momentum_next: bfloat16 [8, 7168, 2048], P(None, ('group', 'shard'))
- update: bfloat16 [8, 7168, 2048], P(None, ('group', 'shard'))
- q_next: bfloat16 [8, 3, 2048, 128], P('group', None, 'shard')
Inputs may be any that keep to these rules, and one draw needn't show every extreme that they name: `owner_group`: each group owns at most 3 experts and some group owns exactly 3; a group's experts fill its slots 0, 1, ... in increasing expert order. `group_counts`: entry g is the number of experts whose owner_group is g, except for one or two groups that own some experts, where it is one less; it equals 3 for some group that owns 3 experts.
All inputs are finite; a program needn't handle non-finite values.
Results may differ from a plain program's by a relative error of at most 0.0059.
Values may be sent and summed in bfloat16 or wider, within the bound.
A program may use at most 128 MiB of HBM per device.

v0:
```python
import math
import jax
import jax.numpy as jnp
from jax import lax
from jax.sharding import PartitionSpec as P

D = 7168
RANK = 128
stability_offset = 1e-06
momentum_decay = 0.6
AXES = ("group", "shard")


def owner_slots(owner_group):
    experts = owner_group.shape[0]
    expert_ids = jnp.arange(experts, dtype=jnp.int32)
    same_owner = owner_group[:, None] == owner_group[None, :]
    earlier = expert_ids[None, :] < expert_ids[:, None]
    return jnp.sum((same_owner & earlier).astype(jnp.int32), axis=1)


def shards(momentum, gradient, q_prev, owner_group, group_counts):
    me = lax.axis_index("group")
    experts, block, hidden = momentum.shape
    cap, share_rows, rank = q_prev.shape[1:]
    slot_of = owner_slots(owner_group)
    keep = slot_of < group_counts[owner_group]
    mine = keep & (owner_group == me)
    pieces = jnp.zeros((experts, share_rows, rank), jnp.bfloat16)
    for j in range(cap):
        pick = mine & (slot_of == j)
        pieces = jnp.where(pick[:, None, None], q_prev[0, j][None], pieces)
    q_one = lax.psum_scatter(pieces, "group", scatter_dimension=0, tiled=True)
    q_shard = lax.all_gather(q_one, "shard", axis=1, tiled=True)
    q_full = lax.all_gather(q_shard, "group", axis=0, tiled=True)
    combined = (momentum.astype(jnp.float32) + gradient.astype(jnp.float32)).astype(jnp.bfloat16)
    left_raw = jnp.einsum("erh,ehk->erk", combined, q_full, preferred_element_type=jnp.float32)
    squares = lax.psum(jnp.sum(left_raw * left_raw, axis=1), AXES)
    left_unit = (left_raw * lax.rsqrt(squares + stability_offset)[:, None, :]).astype(jnp.bfloat16)
    part = jnp.einsum("erh,erk->ehk", combined, left_unit, preferred_element_type=jnp.float32)
    part = lax.psum_scatter(part, "group", scatter_dimension=0, tiled=True)
    share = lax.psum_scatter(part, "shard", scatter_dimension=1, tiled=True)
    right = lax.all_gather(share.astype(jnp.bfloat16), "shard", axis=1, tiled=True)
    right = lax.all_gather(right, "group", axis=0, tiled=True)
    right32 = right.astype(jnp.float32)
    scale = lax.rsqrt(jnp.mean(right32 * right32, axis=1) + stability_offset)
    q_new = (right32 * scale[:, None, :]).astype(jnp.bfloat16)
    update = (
        jnp.einsum("erk,ehk->erh", left_unit, q_new, preferred_element_type=jnp.float32)
        * math.sqrt(D / RANK)
    ).astype(jnp.bfloat16)
    low_rank = jnp.einsum("erk,ehk->erh", left_unit, right, preferred_element_type=jnp.float32)
    momentum_next = (combined.astype(jnp.float32) - (1.0 - momentum_decay) * low_rank).astype(
        jnp.bfloat16
    )
    rows = lax.dynamic_slice_in_dim(q_new, lax.axis_index("shard") * share_rows, share_rows, axis=1)
    kept = []
    for j in range(cap):
        pick = mine & (slot_of == j)
        kept.append(jnp.sum(jnp.where(pick[:, None, None], rows, jnp.zeros_like(rows)), axis=0))
    return (momentum_next, update, jnp.stack(kept)[None])


def solution(mesh):
    return jax.shard_map(
        shards,
        mesh=mesh,
        in_specs=(
            P(None, AXES, None),
            P(None, AXES, None),
            P("group", None, "shard", None),
            P(),
            P(),
        ),
        out_specs=(P(None, AXES, None), P(None, AXES, None), P("group", None, "shard", None)),
        check_vma=False,
    )
```

profile of v0, /device:TPU:0, one launch (start us, length us, event | category | flops | bytes accessed | tf_op | source)
XLA Modules:
  0.0 346.7 jit_solution(16092060516255264329)
XLA Ops:
  7.2 0.0 copy-start
  7.2 0.0 reduce-scatter.4.cloned.1.call-start
  7.2 0.9 convert_reduce_fusion
  8.1 0.7 compare_select_fusion
  8.8 0.0 copy-done
  8.8 0.6 gather_fusion
  9.5 0.7 compare_and_fusion.2
  10.1 1.1 slice_bitcast_fusion.2
  11.2 1.2 select_select_fusion
  12.4 0.0 reduce-scatter.4.cloned.1.call-update
  12.4 0.0 all-gather.3.cloned.1.call-start
  12.5 38.8 %reduce-scatter.4.cloned.1.call-done = bf16[1,512,128]{2,1,0:T(8,128)(2,1)} async-done(((bf16[8,512,128]{2,1,0:T(8,128)(2,1)}), bf16[1,512,128]{2,1,0:T(8,128)(2,1)}) %reduce-scatter.4.cloned.1.call-update) | async-done | bytes 131088 | tf_op jit(solution)/shard_map/reduce_scatter | solution.py:33
  51.3 17.1 %all_gather.12 = bf16[1,2048,128]{2,1,0:T(8,128)(2,1)} all-gather(bf16[1,512,128]{2,1,0:T(8,128)(2,1)} %reduce-scatter.4.cloned.1.call-done), channel_id=1, replica_groups=mesh['group'=8,'shard'=4] {'shard'}, dimensions={1}, use_global_device_ids=true | all-gather | bytes 655360 | tf_op jit(solution)/shard_map/all_gather | solution.py:34
  68.4 0.0 all-gather.3.cloned.1.call-update
  68.4 0.0 reduce-scatter.6.cloned.1.call-start
  68.5 35.9 %all-gather.3.cloned.1.call-done = bf16[8,2048,128]{2,1,0:T(8,128)(2,1)} async-done(((bf16[1,2048,128]{2,1,0:T(8,128)(2,1)}), bf16[8,2048,128]{2,1,0:T(8,128)(2,1)}) %all-gather.3.cloned.1.call-update) | async-done | bytes 4194320 | tf_op jit(solution)/shard_map/all_gather | solution.py:35
  104.4 8.7 %multiply_reduce_fusion = (f32[8,128]{1,0:T(8,128)S(1)}, f32[8,224,128]{2,1,0:T(8,128)S(1)}) fusion(bf16[8,2048,128]{2,1,0:T(8,128)(2,1)} %all-gather.3.cloned.1.call-done, bf16[8,224,2048]{2,1,0:T(8,128)(2,1)} %param.6, bf16[8,224,2048]{2,1,0:T(8,128)(2,1)} %param.5), kind=kOutput, calls=%fused_computation.13 | convolution fusion | flops 954661888 | bytes 19795968 | tf_op jit(solution)/shard_map/erh,ehk->erk/dot_general | solution.py:37
  113.1 39.3 %psum.7 = f32[8,128]{1,0:T(8,128)S(1)} all-reduce(f32[8,128]{1,0:T(8,128)S(1)} %get-tuple-element.13), channel_id=1, replica_groups=mesh['group'=8,'shard'=4] {'group','shard'}, use_global_device_ids=true, to_apply=%region_3.4 | all-reduce | flops 1024 | bytes 8192 | tf_op jit(solution)/shard_map/psum | solution.py:38
  152.4 0.1 multiply_convert_fusion.1
  152.5 11.6 %fusion.3 = f32[8,2048,128]{2,1,0:T(8,128)} fusion(bf16[8,224,128]{2,1,0:T(8,128)(2,1)S(1)} %multiply_convert_fusion.1, bf16[8,224,2048]{2,1,0:T(8,128)(2,1)} %param.6, bf16[8,224,2048]{2,1,0:T(8,128)(2,1)} %param.5), kind=kOutput, calls=%fused_computation.29 | convolution fusion | flops 954204160 | bytes 23527424 | tf_op jit(solution)/shard_map/erh,erk->ehk/dot_general | solution.py:40
  164.1 0.0 reduce-scatter.6.cloned.1.call-update
  164.1 0.0 reduce-scatter.8.cloned.1.call-start
  164.2 72.4 %reduce-scatter.6.cloned.1.call-done = f32[1,2048,128]{2,1,0:T(8,128)} async-done(((f32[8,2048,128]{2,1,0:T(8,128)}), f32[1,2048,128]{2,1,0:T(8,128)}) %reduce-scatter.6.cloned.1.call-update) | async-done | bytes 1048592 | tf_op jit(solution)/shard_map/reduce_scatter | solution.py:41
  236.6 0.0 reduce-scatter.8.cloned.1.call-update
  236.6 0.0 all-gather.5.cloned.1.call-start
  236.6 29.4 %reduce-scatter.8.cloned.1.call-done = f32[1,512,128]{2,1,0:T(8,128)} async-done(((f32[1,2048,128]{2,1,0:T(8,128)}), f32[1,512,128]{2,1,0:T(8,128)}) %reduce-scatter.8.cloned.1.call-update) | async-done | bytes 262160 | tf_op jit(solution)/shard_map/reduce_scatter | solution.py:42
  266.0 1.0 convert_element_type.45
  267.0 16.8 %all_gather.14 = bf16[1,2048,128]{2,1,0:T(8,128)(2,1)} all-gather(bf16[1,512,128]{2,1,0:T(8,128)(2,1)S(1)} %convert_element_type.45), channel_id=1, replica_groups=mesh['group'=8,'shard'=4] {'shard'}, dimensions={1}, use_global_device_ids=true | all-gather | bytes 655360 | tf_op jit(solution)/shard_map/all_gather | solution.py:43
  283.8 0.0 all-gather.5.cloned.1.call-update
  283.8 34.9 %all-gather.5.cloned.1.call-done = bf16[8,2048,128]{2,1,0:T(8,128)(2,1)} async-done(((bf16[1,2048,128]{2,1,0:T(8,128)(2,1)}), bf16[8,2048,128]{2,1,0:T(8,128)(2,1)}) %all-gather.5.cloned.1.call-update) | async-done | bytes 4194320 | tf_op jit(solution)/shard_map/all_gather | solution.py:44
  318.8 3.0 fusion
  321.8 3.1 fusion.1
  324.9 0.0 copy-start.1
  324.9 5.1 %multiply_convert_fusion = bf16[8,224,2048]{2,1,0:T(8,128)(2,1)} fusion(bf16[8,224,128]{2,1,0:T(8,128)(2,1)S(1)} %multiply_convert_fusion.1, bf16[8,2048,128]{2,1,0:T(8,128)(2,1)S(1)} %fusion.1), kind=kOutput, calls=%fused_computation.1 | convolution fusion | flops 946864128 | bytes 11993088 | tf_op jit(solution)/shard_map/erk,ehk->erh/dot_general | solution.py:49
  330.1 0.6 select_reduce_fusion.2
  330.7 0.8 maximum_bitcast_fusion
  331.5 0.0 copy-done.1
  331.5 8.7 %subtract_convert_fusion = bf16[8,224,2048]{2,1,0:T(8,128)(2,1)} fusion(bf16[8,224,128]{2,1,0:T(8,128)(2,1)S(1)} %multiply_convert_fusion.1, bf16[8,2048,128]{2,1,0:T(8,128)(2,1)S(1)} %copy-done.1, bf16[8,224,2048]{2,1,0:T(8,128)(2,1)} %param.6, bf16[8,224,2048]{2,1,0:T(8,128)(2,1)} %param.5), kind=kOutput, calls=%fused_computation.2 | convolution fusion | flops 968884224 | bytes 26673152 | tf_op jit(solution)/shard_map/erk,ehk->erh/dot_general | solution.py:52
  (4 shorter events, 0.0 us)
Async XLA Ops:
  7.2 1.6 copy-start
  7.2 44.1 %reduce-scatter.4.cloned.1.call-start = ((), (), s32[]{:S(2)}) async-start(), calls=%async_computation.3 | async-start | bytes 1179648 | tf_op jit(solution)/shard_map/reduce_scatter | solution.py:33
  12.4 91.9 %all-gather.3.cloned.1.call-start = ((), (), s32[]{:S(2)}) async-start(), calls=%async_computation.4 | async-start | bytes 4718592 | tf_op jit(solution)/shard_map/all_gather | solution.py:35
  68.4 168.1 %reduce-scatter.6.cloned.1.call-start = ((), (), s32[]{:S(2)}) async-start(), calls=%async_computation.5 | async-start | bytes 9437184 | tf_op jit(solution)/shard_map/reduce_scatter | solution.py:41
  164.1 101.9 %reduce-scatter.8.cloned.1.call-start = ((), (), s32[]{:S(2)}) async-start(), calls=%async_computation.6 | async-start | bytes 1310720 | tf_op jit(solution)/shard_map/reduce_scatter | solution.py:42
  236.6 82.2 %all-gather.5.cloned.1.call-start = ((), (), s32[]{:S(2)}) async-start(), calls=%async_computation.7 | async-start | bytes 4718592 | tf_op jit(solution)/shard_map/all_gather | solution.py:44
  324.9 6.6 %copy-start.1 = (bf16[8,2048,128]{2,1,0:T(8,128)(2,1)S(1)}, bf16[8,2048,128]{2,1,0:T(8,128)(2,1)}, u32[]{:S(2)}) copy-start(bf16[8,2048,128]{2,1,0:T(8,128)(2,1)} %all-gather.5.cloned.1.call-done) | copy-start | bytes 12582916
Sparse Core Ops, SparseCore 0:
  12.5 38.6 reduce-scatter.3
  68.5 35.7 all-gather.2
  164.3 72.2 reduce-scatter.5
  238.7 27.2 reduce-scatter.7
  283.9 34.7 all-gather.4
where the time goes:
time: 347 us
  waiting for transfers between devices  211 us (61%)
  blocking collectives  73.3 us (21%)
  matrix products  34.2 us (10%)
  between operations  13.8 us (4%)
  other arithmetic  12.1 us (3%)
    reduce_scatter x1, waiting for transfers between devices, shards(): part = lax.psum_scatter(part, 'group', scatter_dimension=0, tiled=True)  72.4 us
    psum x1, blocking collectives, shards(): squares = lax.psum(jnp.sum(left_raw * left_raw, axis=1), AXES)  39.3 us
    reduce_scatter x1, waiting for transfers between devices, shards(): q_one = lax.psum_scatter(pieces, 'group', scatter_dimension=0, tiled=True)  38.8 us
    all_gather x1, waiting for transfers between devices, shards(): q_full = lax.all_gather(q_shard, 'group', axis=0, tiled=True)  35.9 us
    all_gather x1, waiting for transfers between devices, shards(): right = lax.all_gather(right, 'group', axis=0, tiled=True)  34.9 us
    reduce_scatter x1, waiting for transfers between devices, shards(): share = lax.psum_scatter(part, 'shard', scatter_dimension=1, tiled=True)  29.4 us
    all_gather x1, blocking collectives, shards(): q_shard = lax.all_gather(q_one, 'shard', axis=1, tiled=True)  17.1 us
    all_gather x1, blocking collectives, shards(): lax.all_gather(share.astype(jnp.bfloat16), 'shard', axis=1, tiled=True)  16.8 us
  transfers between devices with their start and end apart: 5, of which 5 were waited for; matrix products, arithmetic and copies ran while one was open for 0% of the time, Pallas kernels for 0%

commit v1 on v0

--- a/solution.py
+++ b/solution.py
@@ -35,7 +35,9 @@
     q_full = lax.all_gather(q_shard, "group", axis=0, tiled=True)
     combined = (momentum.astype(jnp.float32) + gradient.astype(jnp.float32)).astype(jnp.bfloat16)
     left_raw = jnp.einsum("erh,ehk->erk", combined, q_full, preferred_element_type=jnp.float32)
-    squares = lax.psum(jnp.sum(left_raw * left_raw, axis=1), AXES)
+    block_2 = jnp.sum(left_raw * left_raw, axis=1)
+    blocks = lax.all_gather(block_2, AXES)
+    squares = jnp.sum(blocks, axis=0)
     left_unit = (left_raw * lax.rsqrt(squares + stability_offset)[:, None, :]).astype(jnp.bfloat16)
     part = jnp.einsum("erh,erk->ehk", combined, left_unit, preferred_element_type=jnp.float32)
     part = lax.psum_scatter(part, "group", scatter_dimension=0, tiled=True)

time: 347 us -> 373 us (1.075)
  blocking collectives: 73.3 us -> 102 us
    all_gather x0 -> x1, blocking collectives: none -> 68.4 us  [shards(): blocks = lax.all_gather(block_2, AXES)]
    psum x1 -> x0, blocking collectives: 39.3 us -> none  [shards(): squares = lax.psum(jnp.sum(left_raw * left_raw, axis=1), AXES)]
where the time goes in v1:
time: 373 us; the launch traced here: 372 us
  waiting for transfers between devices  208 us (56%)
  blocking collectives  102 us (27%)
  matrix products  34.2 us (9%)
  between operations  13.8 us (4%)
  other arithmetic  12.1 us (3%)
    reduce_scatter x1, waiting for transfers between devices, shards(): part = lax.psum_scatter(part, 'group', scatter_dimension=0, tiled=True)  68.9 us
    all_gather x1, blocking collectives, shards(): blocks = lax.all_gather(block_2, AXES)  68.4 us
    reduce_scatter x1, waiting for transfers between devices, shards(): q_one = lax.psum_scatter(pieces, 'group', scatter_dimension=0, tiled=True)  38.8 us
    all_gather x1, waiting for transfers between devices, shards(): q_full = lax.all_gather(q_shard, 'group', axis=0, tiled=True)  35.9 us
    all_gather x1, waiting for transfers between devices, shards(): right = lax.all_gather(right, 'group', axis=0, tiled=True)  35 us
    reduce_scatter x1, waiting for transfers between devices, shards(): share = lax.psum_scatter(part, 'shard', scatter_dimension=1, tiled=True)  29.4 us
    all_gather x1, blocking collectives, shards(): q_shard = lax.all_gather(q_one, 'shard', axis=1, tiled=True)  17.1 us
    all_gather x1, blocking collectives, shards(): lax.all_gather(share.astype(jnp.bfloat16), 'shard', axis=1, tiled=True)  16.8 us
  transfers between devices with their start and end apart: 5, of which 5 were waited for; matrix products, arithmetic and copies ran while one was open for 0% of the time, Pallas kernels for 0%

profile of v1, /device:TPU:0, one launch (start us, length us, event | category | flops | bytes accessed | tf_op | source)
XLA Modules:
  0.0 372.3 jit_solution(12797015611868373413)
XLA Ops:
  7.2 0.0 copy-start
  7.2 0.0 reduce-scatter.4.cloned.1.call-start
  7.2 0.9 convert_reduce_fusion
  8.1 0.7 compare_select_fusion
  8.8 0.0 copy-done
  8.8 0.6 gather_fusion
  9.5 0.7 compare_and_fusion.2
  10.1 1.1 slice_bitcast_fusion.2
  11.2 1.2 select_select_fusion
  12.4 0.0 reduce-scatter.4.cloned.1.call-update
  12.4 0.0 all-gather.4.cloned.1.call-start
  12.5 38.8 %reduce-scatter.4.cloned.1.call-done = bf16[1,512,128]{2,1,0:T(8,128)(2,1)} async-done(((bf16[8,512,128]{2,1,0:T(8,128)(2,1)}), bf16[1,512,128]{2,1,0:T(8,128)(2,1)}) %reduce-scatter.4.cloned.1.call-update) | async-done | bytes 131088 | tf_op jit(solution)/shard_map/reduce_scatter | solution.py:33
  51.3 17.1 %all_gather.18 = bf16[1,2048,128]{2,1,0:T(8,128)(2,1)} all-gather(bf16[1,512,128]{2,1,0:T(8,128)(2,1)} %reduce-scatter.4.cloned.1.call-done), channel_id=1, replica_groups=mesh['group'=8,'shard'=4] {'shard'}, dimensions={1}, use_global_device_ids=true | all-gather | bytes 655360 | tf_op jit(solution)/shard_map/all_gather | solution.py:34
  68.4 0.0 all-gather.4.cloned.1.call-update
  68.4 0.0 reduce-scatter.6.cloned.1.call-start
  68.5 35.9 %all-gather.4.cloned.1.call-done = bf16[8,2048,128]{2,1,0:T(8,128)(2,1)} async-done(((bf16[1,2048,128]{2,1,0:T(8,128)(2,1)}), bf16[8,2048,128]{2,1,0:T(8,128)(2,1)}) %all-gather.4.cloned.1.call-update) | async-done | bytes 4194320 | tf_op jit(solution)/shard_map/all_gather | solution.py:35
  104.4 8.7 %multiply_reduce_fusion = (f32[8,128]{1,0:T(8,128)S(1)}, f32[8,224,128]{2,1,0:T(8,128)S(1)}) fusion(bf16[8,2048,128]{2,1,0:T(8,128)(2,1)} %all-gather.4.cloned.1.call-done, bf16[8,224,2048]{2,1,0:T(8,128)(2,1)} %param.6, bf16[8,224,2048]{2,1,0:T(8,128)(2,1)} %param.5), kind=kOutput, calls=%fused_computation.13 | convolution fusion | flops 954661888 | bytes 19795968 | tf_op jit(solution)/shard_map/erh,ehk->erk/dot_general | solution.py:37
  113.1 68.4 %all-gather = f32[256,128]{1,0:T(8,128)S(1)} all-gather(f32[8,128]{1,0:T(8,128)S(1)} %get-tuple-element.13), channel_id=2, replica_groups=mesh['group'=8,'shard'=4] {'group','shard'}, dimensions={0}, use_global_device_ids=true | all-gather | bytes 135168 | tf_op jit(solution)/shard_map/all_gather | solution.py:39
  181.5 0.1 multiply_convert_fusion.1
  181.6 11.6 %fusion.3 = f32[8,2048,128]{2,1,0:T(8,128)} fusion(bf16[8,224,128]{2,1,0:T(8,128)(2,1)S(1)} %multiply_convert_fusion.1, bf16[8,224,2048]{2,1,0:T(8,128)(2,1)} %param.6, bf16[8,224,2048]{2,1,0:T(8,128)(2,1)} %param.5), kind=kOutput, calls=%fused_computation.30 | convolution fusion | flops 954204160 | bytes 23527424 | tf_op jit(solution)/shard_map/erh,erk->ehk/dot_general | solution.py:42
  193.2 0.0 reduce-scatter.6.cloned.1.call-update
  193.2 0.0 reduce-scatter.8.cloned.1.call-start
  193.3 68.9 %reduce-scatter.6.cloned.1.call-done = f32[1,2048,128]{2,1,0:T(8,128)} async-done(((f32[8,2048,128]{2,1,0:T(8,128)}), f32[1,2048,128]{2,1,0:T(8,128)}) %reduce-scatter.6.cloned.1.call-update) | async-done | bytes 1048592 | tf_op jit(solution)/shard_map/reduce_scatter | solution.py:43
  262.1 0.0 reduce-scatter.8.cloned.1.call-update
  262.2 0.0 all-gather.6.cloned.1.call-start
  262.2 29.4 %reduce-scatter.8.cloned.1.call-done = f32[1,512,128]{2,1,0:T(8,128)} async-done(((f32[1,2048,128]{2,1,0:T(8,128)}), f32[1,512,128]{2,1,0:T(8,128)}) %reduce-scatter.8.cloned.1.call-update) | async-done | bytes 262160 | tf_op jit(solution)/shard_map/reduce_scatter | solution.py:44
  291.6 1.0 convert_element_type.45
  292.5 16.8 %all_gather.22 = bf16[1,2048,128]{2,1,0:T(8,128)(2,1)} all-gather(bf16[1,512,128]{2,1,0:T(8,128)(2,1)S(1)} %convert_element_type.45), channel_id=1, replica_groups=mesh['group'=8,'shard'=4] {'shard'}, dimensions={1}, use_global_device_ids=true | all-gather | bytes 655360 | tf_op jit(solution)/shard_map/all_gather | solution.py:45
  309.4 0.0 all-gather.6.cloned.1.call-update
  309.4 35.0 %all-gather.6.cloned.1.call-done = bf16[8,2048,128]{2,1,0:T(8,128)(2,1)} async-done(((bf16[1,2048,128]{2,1,0:T(8,128)(2,1)}), bf16[8,2048,128]{2,1,0:T(8,128)(2,1)}) %all-gather.6.cloned.1.call-update) | async-done | bytes 4194320 | tf_op jit(solution)/shard_map/all_gather | solution.py:46
  344.3 3.0 fusion
  347.4 3.1 fusion.1
  350.5 0.0 copy-start.1
  350.5 5.1 %multiply_convert_fusion = bf16[8,224,2048]{2,1,0:T(8,128)(2,1)} fusion(bf16[8,224,128]{2,1,0:T(8,128)(2,1)S(1)} %multiply_convert_fusion.1, bf16[8,2048,128]{2,1,0:T(8,128)(2,1)S(1)} %fusion.1), kind=kOutput, calls=%fused_computation.1 | convolution fusion | flops 946864128 | bytes 11993088 | tf_op jit(solution)/shard_map/erk,ehk->erh/dot_general | solution.py:51
  355.6 0.6 select_reduce_fusion.2
  356.3 0.8 maximum_bitcast_fusion
  357.1 0.0 copy-done.1
  357.1 8.7 %subtract_convert_fusion = bf16[8,224,2048]{2,1,0:T(8,128)(2,1)} fusion(bf16[8,224,128]{2,1,0:T(8,128)(2,1)S(1)} %multiply_convert_fusion.1, bf16[8,2048,128]{2,1,0:T(8,128)(2,1)S(1)} %copy-done.1, bf16[8,224,2048]{2,1,0:T(8,128)(2,1)} %param.6, bf16[8,224,2048]{2,1,0:T(8,128)(2,1)} %param.5), kind=kOutput, calls=%fused_computation.2 | convolution fusion | flops 968884224 | bytes 26673152 | tf_op jit(solution)/shard_map/erk,ehk->erh/dot_general | solution.py:54
  (5 shorter events, 0.1 us)
Async XLA Ops:
  7.2 1.6 copy-start
  7.2 44.1 %reduce-scatter.4.cloned.1.call-start = ((), (), s32[]{:S(2)}) async-start(), calls=%async_computation.3 | async-start | bytes 1179648 | tf_op jit(solution)/shard_map/reduce_scatter | solution.py:33
  12.4 91.9 %all-gather.4.cloned.1.call-start = ((), (), s32[]{:S(2)}) async-start(), calls=%async_computation.4 | async-start | bytes 4718592 | tf_op jit(solution)/shard_map/all_gather | solution.py:35
  68.4 193.7 %reduce-scatter.6.cloned.1.call-start = ((), (), s32[]{:S(2)}) async-start(), calls=%async_computation.5 | async-start | bytes 9437184 | tf_op jit(solution)/shard_map/reduce_scatter | solution.py:43
  193.2 98.3 %reduce-scatter.8.cloned.1.call-start = ((), (), s32[]{:S(2)}) async-start(), calls=%async_computation.6 | async-start | bytes 1310720 | tf_op jit(solution)/shard_map/reduce_scatter | solution.py:44
  262.2 82.2 %all-gather.6.cloned.1.call-start = ((), (), s32[]{:S(2)}) async-start(), calls=%async_computation.7 | async-start | bytes 4718592 | tf_op jit(solution)/shard_map/all_gather | solution.py:46
  350.5 6.6 %copy-start.1 = (bf16[8,2048,128]{2,1,0:T(8,128)(2,1)S(1)}, bf16[8,2048,128]{2,1,0:T(8,128)(2,1)}, u32[]{:S(2)}) copy-start(bf16[8,2048,128]{2,1,0:T(8,128)(2,1)} %all-gather.6.cloned.1.call-done) | copy-start | bytes 12582916
Sparse Core Ops, SparseCore 0:
  12.5 38.6 reduce-scatter.3
  68.5 35.7 all-gather.3
  193.4 68.7 reduce-scatter.5
  264.3 27.2 reduce-scatter.7
  309.5 34.7 all-gather.5
